TPU v7x, 32 devices: a whole 2x2x4 slice. The times are simulated.
32 devices in a mesh: frames: 8 (over z, x), rows: 4 (over y, core).
Axes of the slice: x: 2, y: 2, z: 4, core: 2. Of those that a mesh axis runs over, the one named last changes fastest.
Arguments:
- fmap: bfloat16 [16, 12, 64, 128], P('frames', 'rows'), may hold values from -6 to 6
- context: bfloat16 [16, 12, 64, 128], P('frames', 'rows'), may hold values from -6 to 6
- pairs: int32 [32, 3], replicated, may hold values from 0 to 15, as said below
- w_corr: bfloat16 [49, 128], replicated, may hold values from -0.875 to 0.875
- w_zr: bfloat16 [256, 256], replicated, may hold values from -0.375 to 0.375
- w_q: bfloat16 [9, 256, 128], replicated, may hold values from -0.125 to 0.125
- w_msg: bfloat16 [128, 256], replicated, may hold values from -0.5 to 0.5
- w_res: bfloat16 [9, 128, 128], replicated, may hold values from -0.1875 to 0.1875
Outputs:
- state: bfloat16 [16, 12, 64, 128], P('frames', 'rows')
Inputs may be any that keep to these rules, and one draw needn't show every extreme that they name: Source and target differ. With dev(f) = f // 2, the source's dev, the target's dev and the owner differ pairwise by at most one. No owner holds more than 8 pairs, and some owner holds exactly 8.
All inputs are finite; a program needn't handle non-finite values.
Results may differ from a plain program's by a relative error of at most 0.01.
Values may be sent and summed in bfloat16 or wider, within the bound.
A program may use at most 64 MiB of HBM per device.

v0:
```python
import jax
import jax.numpy as jnp
from jax import lax
from jax.sharding import PartitionSpec as P

RADIUS = 3
ROUNDS = 2
CAPACITY = 8


def with_halo(array, sides, width):
    for axis, dim in sides:
        size, length = (lax.axis_size(axis), array.shape[dim])
        up = [(i, (i + 1) % size) for i in range(size - 1)]
        down = [(j, i) for i, j in up]
        last = lax.slice_in_dim(array, length - width, length, axis=dim)
        leading = lax.slice_in_dim(array, 0, width, axis=dim)
        before = lax.ppermute(last, axis, up)
        after = lax.ppermute(leading, axis, down)
        array = jnp.concatenate([before, array, after], axis=dim)
    return array


def passed_along(block, axis, distance):
    devices = range(lax.axis_size(axis))
    route = [(i - distance, i) for i in devices if i - distance in devices]
    return lax.ppermute(block, axis, route)


def slot_table(pair_rows, owner_index):
    owners = pair_rows[:, 2]
    mine = (owners == owner_index).astype(jnp.int32)
    ranks = jnp.cumsum(mine) - mine
    levels = jnp.arange(CAPACITY, dtype=jnp.int32)
    picks = mine[None, :] * (ranks[None, :] == levels[:, None]).astype(jnp.int32)
    sources = jnp.sum(picks * pair_rows[None, :, 0], axis=1)
    targets = jnp.sum(picks * pair_rows[None, :, 1], axis=1)
    valid = jnp.sum(picks, axis=1)
    return (sources, targets, valid)


def dest_onehot(frame_ids, valid, start, count):
    relative = frame_ids - start
    inside = valid * (relative >= 0).astype(jnp.int32) * (relative < count).astype(jnp.int32)
    levels = jnp.arange(count, dtype=jnp.int32)
    hits = (relative[None, :] == levels[:, None]).astype(jnp.int32) * inside[None, :]
    return hits.astype(jnp.bfloat16)


def conv_taps(padded, kernel, height, width):
    count = padded.shape[0]
    cin = padded.shape[-1]
    total = None
    for row_off in range(3):
        for col_off in range(3):
            window = padded[:, row_off : row_off + height, col_off : col_off + width, :].reshape(
                -1, cin
            )
            term = jnp.dot(
                window, kernel[3 * row_off + col_off], preferred_element_type=jnp.float32
            )
            total = term if total is None else total + term
    return total.reshape(count, height, width, -1)


def pad_columns(field, amount):
    return jnp.pad(field, ((0, 0), (0, 0), (amount, amount), (0, 0)))


def spread_messages(messages, sources, targets, valid, start, count):
    chans = messages.shape[-1] // 2
    slots = messages.shape[0]
    first_half = messages[..., :chans].reshape(slots, -1)
    second_half = messages[..., chans:].reshape(slots, -1)
    to_source = dest_onehot(sources, valid, start, count)
    to_target = dest_onehot(targets, valid, start, count)
    return jnp.dot(to_source, first_half, preferred_element_type=jnp.float32) + jnp.dot(
        to_target, second_half, preferred_element_type=jnp.float32
    )


def local(fmap, context, pairs, w_corr, w_zr, w_q, w_msg, w_res):
    frame_dev, height, width, chans = fmap.shape
    own_index = lax.axis_index("frames")
    sources, targets, valid = slot_table(pairs, own_index)
    feat_window = with_halo(fmap, (("frames", 0),), frame_dev)
    window_start = (own_index - 1) * frame_dev
    limit = feat_window.shape[0] - 1
    src_index = jnp.clip(sources - window_start, 0, limit)
    tgt_index = jnp.clip(targets - window_start, 0, limit)
    src_feat = jnp.take(feat_window, src_index, axis=0)
    tgt_feat = jnp.take(feat_window, tgt_index, axis=0)
    tgt_rim = with_halo(tgt_feat, (("rows", 1),), RADIUS)
    tgt_rim = pad_columns(tgt_rim, RADIUS)
    span = 2 * RADIUS + 1
    columns = []
    for row_off in range(span):
        for col_off in range(span):
            moved = tgt_rim[:, row_off : row_off + height, col_off : col_off + width, :]
            columns.append(
                jnp.einsum("syxc,syxc->syx", src_feat, moved, preferred_element_type=jnp.float32)
            )
    scale = 1.0 / chans**0.5
    corr = (jnp.stack(columns, axis=-1) * scale).astype(jnp.bfloat16)
    motion = jax.nn.relu(
        jnp.dot(corr.reshape(-1, span * span), w_corr, preferred_element_type=jnp.float32)
    )
    motion = motion.astype(jnp.bfloat16).reshape(-1, height, width, chans)
    slots = motion.shape[0]
    state = context
    hidden = None
    for sweep in range(ROUNDS):
        state_window = with_halo(state, (("frames", 0),), frame_dev)
        ctx_src = jnp.take(state_window, src_index, axis=0).astype(jnp.float32)
        if sweep == 0:
            hidden = jnp.tanh(ctx_src)
        xin = (motion.astype(jnp.float32) + ctx_src).astype(jnp.bfloat16)
        joined = jnp.concatenate([hidden.astype(jnp.bfloat16), xin], axis=-1)
        gates = jax.nn.sigmoid(
            jnp.dot(joined.reshape(-1, 2 * chans), w_zr, preferred_element_type=jnp.float32)
        )
        gates = gates.reshape(slots, height, width, 2 * chans)
        update_gate = gates[..., :chans]
        reset_gate = gates[..., chans:]
        qin = jnp.concatenate([(reset_gate * hidden).astype(jnp.bfloat16), xin], axis=-1)
        qin_rim = pad_columns(with_halo(qin, (("rows", 1),), 1), 1)
        candidate = jnp.tanh(conv_taps(qin_rim, w_q, height, width))
        hidden = (1.0 - update_gate) * hidden + update_gate * candidate
        messages = jnp.dot(
            hidden.astype(jnp.bfloat16).reshape(-1, chans),
            w_msg,
            preferred_element_type=jnp.float32,
        )
        messages = messages.astype(jnp.bfloat16).reshape(slots, height, width, 2 * chans)
        partial_value = spread_messages(
            messages, sources, targets, valid, (own_index - 1) * frame_dev, 3 * frame_dev
        )
        incoming = partial_value[frame_dev : 2 * frame_dev]
        for offset, piece in ((-1, partial_value[:frame_dev]), (1, partial_value[2 * frame_dev :])):
            incoming = incoming + passed_along(piece.astype(jnp.bfloat16), "frames", offset).astype(
                piece.dtype
            )
        update = jax.nn.relu(incoming).reshape(frame_dev, height, width, chans).astype(jnp.bfloat16)
        update_rim = pad_columns(with_halo(update, (("rows", 1),), 1), 1)
        state = (state.astype(jnp.float32) + conv_taps(update_rim, w_res, height, width)).astype(
            jnp.bfloat16
        )
    return state


def solution(mesh):
    placed = (
        P("frames", "rows", None, None),
        P("frames", "rows", None, None),
        P(),
        P(),
        P(),
        P(),
        P(),
        P(),
    )
    return jax.shard_map(
        local,
        mesh=mesh,
        in_specs=placed,
        out_specs=P("frames", "rows", None, None),
        check_vma=False,
    )
```

profile of v0, /device:TPU:14, one launch (start us, length us, event | category | flops | bytes accessed | tf_op | source)
XLA Modules:
  0.0 135.0 jit_solution(16281709327165662875)
XLA Ops:
  0.0 2.6 %collective-permute-start.1 = (bf16[2,3,64,128]{3,2,1,0:T(8,128)(2,1)}, bf16[2,3,64,128]{3,2,1,0:T(8,128)(2,1)S(1)}, u32[]{:S(2)}, u32[]{:S(2)}) collective-permute-start(bf16[2,3,64,128]{3,2,1,0:T(8,128)(2,1)} %param.11), channel_id=1, source_target_pairs={{4,0},{8,4},{12,8},{16,12},{20,16},{24,20},{28,24},{5,1},{9,5},{13... | collective-permute-start | bytes 294920 | tf_op jit(solution)/shard_map/ppermute | solution.py:19
  2.6 4.3 %collective-permute-start = (bf16[2,3,64,128]{3,2,1,0:T(8,128)(2,1)}, bf16[2,3,64,128]{3,2,1,0:T(8,128)(2,1)S(1)}, u32[]{:S(2)}, u32[]{:S(2)}) collective-permute-start(bf16[2,3,64,128]{3,2,1,0:T(8,128)(2,1)} %param.11), channel_id=1, source_target_pairs={{0,4},{4,8},{8,12},{12,16},{16,20},{20,24},{24,28},{1,5},{5,9},{9,... | collective-permute-start | bytes 294920 | tf_op jit(solution)/shard_map/ppermute | solution.py:18
  6.9 2.6 %collective-permute-start.2 = (bf16[2,3,64,128]{3,2,1,0:T(8,128)(2,1)}, bf16[2,3,64,128]{3,2,1,0:T(8,128)(2,1)S(1)}, u32[]{:S(2)}, u32[]{:S(2)}) collective-permute-start(bf16[2,3,64,128]{3,2,1,0:T(8,128)(2,1)} %param.10), channel_id=1, source_target_pairs={{0,4},{4,8},{8,12},{12,16},{16,20},{20,24},{24,28},{1,5},{5,9},{9,... | collective-permute-start | bytes 294920 | tf_op jit(solution)/shard_map/ppermute | solution.py:18
  9.4 3.3 %collective-permute-start.3 = (bf16[2,3,64,128]{3,2,1,0:T(8,128)(2,1)}, bf16[2,3,64,128]{3,2,1,0:T(8,128)(2,1)S(1)}, u32[]{:S(2)}, u32[]{:S(2)}) collective-permute-start(bf16[2,3,64,128]{3,2,1,0:T(8,128)(2,1)} %param.10), channel_id=1, source_target_pairs={{4,0},{8,4},{12,8},{16,12},{20,16},{24,20},{28,24},{5,1},{9,5},{13... | collective-permute-start | bytes 294920 | tf_op jit(solution)/shard_map/ppermute | solution.py:19
  12.7 0.7 fusion.263
  13.4 0.7 compare_convert_fusion
  14.1 0.8 slice_bitcast_fusion
  15.1 0.7 bitcast_subtract_fusion
  16.1 0.9 constant_dynamic-update-slice_fusion.1
  17.1 0.6 gather_fusion.2
  17.8 1.9 %collective-permute-start.5 = (bf16[8,3,64,128]{3,2,1,0:T(8,128)(2,1)S(1)}, bf16[8,3,64,128]{3,2,1,0:T(8,128)(2,1)S(1)}, u32[]{:S(2)}, u32[]{:S(2)}) collective-permute-start(bf16[8,3,64,128]{3,2,1,0:T(8,128)(2,1)S(1)} %broadcast_select_fusion), channel_id=1, source_target_pairs={{1,0},{2,1},{3,2},{5,4},{6,5},{7,6},{9,8},{10,9},{11,10},{13,12},{... | collective-permute-start | bytes 1179656 | tf_op jit(solution)/shard_map/ppermute | solution.py:19
  19.8 2.4 %collective-permute-start.4 = (bf16[8,3,64,128]{3,2,1,0:T(8,128)(2,1)S(1)}, bf16[8,3,64,128]{3,2,1,0:T(8,128)(2,1)S(1)}, u32[]{:S(2)}, u32[]{:S(2)}) collective-permute-start(bf16[8,3,64,128]{3,2,1,0:T(8,128)(2,1)S(1)} %broadcast_select_fusion), channel_id=1, source_target_pairs={{0,1},{1,2},{2,3},{4,5},{5,6},{6,7},{8,9},{9,10},{10,11},{12,13},{... | collective-permute-start | bytes 1179656 | tf_op jit(solution)/shard_map/ppermute | solution.py:18
  22.2 0.6 gather_fusion.1
  22.9 0.6 gather_fusion
  23.6 1.5 %collective-permute-done.5 = bf16[8,3,64,128]{3,2,1,0:T(8,128)(2,1)S(1)} collective-permute-done((bf16[8,3,64,128]{3,2,1,0:T(8,128)(2,1)S(1)}, bf16[8,3,64,128]{3,2,1,0:T(8,128)(2,1)S(1)}, u32[]{:S(2)}, u32[]{:S(2)}) %collective-permute-start.5) | collective-permute-done | bytes 393248 | tf_op jit(solution)/shard_map/ppermute | solution.py:19
  25.0 3.8 %collective-permute-done.4 = bf16[8,3,64,128]{3,2,1,0:T(8,128)(2,1)S(1)} collective-permute-done((bf16[8,3,64,128]{3,2,1,0:T(8,128)(2,1)S(1)}, bf16[8,3,64,128]{3,2,1,0:T(8,128)(2,1)S(1)}, u32[]{:S(2)}, u32[]{:S(2)}) %collective-permute-start.4) | collective-permute-done | bytes 393248 | tf_op jit(solution)/shard_map/ppermute | solution.py:18
  28.9 0.7 fusion.20
  29.5 2.0 %fusion.38 = (f32[8,3,64]{2,1,0:T(4,128)S(1)}, f32[8,3,64]{2,1,0:T(4,128)S(1)}, f32[8,3,64]{2,1,0:T(4,128)S(1)}, f32[8,3,64]{2,1,0:T(4,128)S(1)}, f32[8,3,64]{2,...) fusion(bf16[8,9,70,128]{3,2,1,0:T(8,128)(2,1)S(1)} %fusion.20, ...), kind=kLoop, calls=%fused_computation.150 | loop fusion | flops 5099520 | bytes 3588104 | tf_op jit(solution)/shard_map/syxc,syxc->syx/dot_general | solution.py:101
  31.5 3.9 %fusion.58 = (f32[8,3,64]{2,1,0:T(4,128)S(1)}, f32[8,3,64]{2,1,0:T(4,128)S(1)}, f32[8,3,64]{2,1,0:T(4,128)S(1)}, f32[8,3,64]{2,1,0:T(4,128)S(1)}, f32[8,3,64]{2,...) fusion(bf16[8,9,70,128]{3,2,1,0:T(8,128)(2,1)S(1)} %fusion.20, ...), kind=kLoop, calls=%fused_computation.170 | loop fusion | flops 10394112 | bytes 7182344 | tf_op jit(solution)/shard_map/syxc,syxc->syx/dot_general | solution.py:101
  35.4 3.9 %fusion.78 = (f32[8,3,64]{2,1,0:T(4,128)S(1)}, f32[8,3,64]{2,1,0:T(4,128)S(1)}, f32[8,3,64]{2,1,0:T(4,128)S(1)}, f32[8,3,64]{2,1,0:T(4,128)S(1)}, f32[8,3,64]{2,...) fusion(bf16[8,9,70,128]{3,2,1,0:T(8,128)(2,1)S(1)} %fusion.20, ...), kind=kLoop, calls=%fused_computation.190 | loop fusion | flops 10394112 | bytes 7182344 | tf_op jit(solution)/shard_map/syxc,syxc->syx/dot_general | solution.py:101
  39.7 1.7 %fusion.68 = (f32[8,3,64]{2,1,0:T(4,128)S(1)}, f32[8,3,64]{2,1,0:T(4,128)S(1)}, f32[8,3,64]{2,1,0:T(4,128)S(1)}, f32[8,3,64]{2,1,0:T(4,128)S(1)}, f32[8,3,64]{2,...) fusion(bf16[8,3,64,128]{3,2,1,0:T(8,128)(2,1)S(1)} %collective-permute-done.5, ...), kind=kLoop, calls=%fused_computation.180 | loop fusion | flops 5297664 | bytes 1615880 | tf_op jit(solution)/shard_map/syxc,syxc->syx/dot_general | solution.py:101
  45.4 0.5 stack.199
  46.6 0.6 fusion.6
  47.5 1.9 %collective-permute-start.7 = (bf16[8,1,64,256]{3,2,1,0:T(8,128)(2,1)S(1)}, bf16[8,1,64,256]{3,2,1,0:T(8,128)(2,1)S(1)}, u32[]{:S(2)}, u32[]{:S(2)}) collective-permute-start(bf16[8,1,64,256]{3,2,1,0:T(8,128)(2,1)S(1)} %get-tuple-element.95), channel_id=1, source_target_pairs={{1,0},{2,1},{3,2},{5,4},{6,5},{7,6},{9,8},{10,9},{11,10},{13,12},{... | collective-permute-start | bytes 786440 | tf_op jit(solution)/shard_map/ppermute | solution.py:19
  49.4 2.6 %collective-permute-start.6 = (bf16[8,1,64,256]{3,2,1,0:T(8,128)(2,1)S(1)}, bf16[8,1,64,256]{3,2,1,0:T(8,128)(2,1)S(1)}, u32[]{:S(2)}, u32[]{:S(2)}) collective-permute-start(bf16[8,1,64,256]{3,2,1,0:T(8,128)(2,1)S(1)} %get-tuple-element.94), channel_id=1, source_target_pairs={{0,1},{1,2},{2,3},{4,5},{5,6},{6,7},{8,9},{9,10},{10,11},{12,13},{... | collective-permute-start | bytes 786440 | tf_op jit(solution)/shard_map/ppermute | solution.py:18
  52.0 1.3 collective-permute-done.7
  53.3 3.8 %collective-permute-done.6 = bf16[8,1,64,256]{3,2,1,0:T(8,128)(2,1)S(1)} collective-permute-done((bf16[8,1,64,256]{3,2,1,0:T(8,128)(2,1)S(1)}, bf16[8,1,64,256]{3,2,1,0:T(8,128)(2,1)S(1)}, u32[]{:S(2)}, u32[]{:S(2)}) %collective-permute-start.6) | collective-permute-done | bytes 262176 | tf_op jit(solution)/shard_map/ppermute | solution.py:18
  57.1 0.9 select_maximum_fusion.3
  58.0 1.0 fusion.207
  60.5 0.4 convolution_add_fusion.14
  60.9 0.4 convolution_add_fusion.13
  61.2 0.4 convolution_add_fusion.12
  62.0 0.4 convolution_add_fusion.10
  62.3 0.4 fusion.11
  63.0 0.5 copy-done.5
  65.0 3.4 %collective-permute-start.9 = (bf16[2,24576]{1,0:T(2,128)(2,1)S(1)}, bf16[2,24576]{1,0:T(2,128)(2,1)S(1)}, u32[]{:S(2)}, u32[]{:S(2)}) collective-permute-start(bf16[2,24576]{1,0:T(2,128)(2,1)S(1)} %get-tuple-element.101), channel_id=1, source_target_pairs={{0,4},{4,8},{8,12},{12,16},{16,20},{20,24},{24,28},{1,5},{5,9},{9,... | collective-permute-start | bytes 294920 | tf_op jit(solution)/shard_map/ppermute | solution.py:27
  68.4 2.4 %collective-permute-start.8 = (bf16[2,24576]{1,0:T(2,128)(2,1)S(1)}, bf16[2,24576]{1,0:T(2,128)(2,1)S(1)}, u32[]{:S(2)}, u32[]{:S(2)}) collective-permute-start(bf16[2,24576]{1,0:T(2,128)(2,1)S(1)} %get-tuple-element.100), channel_id=1, source_target_pairs={{4,0},{8,4},{12,8},{16,12},{20,16},{24,20},{28,24},{5,1},{9,5},{13... | collective-permute-start | bytes 294920 | tf_op jit(solution)/shard_map/ppermute | solution.py:27
  70.9 1.0 collective-permute-done.9
  71.9 3.9 %collective-permute-done.8 = bf16[2,24576]{1,0:T(2,128)(2,1)S(1)} collective-permute-done((bf16[2,24576]{1,0:T(2,128)(2,1)S(1)}, bf16[2,24576]{1,0:T(2,128)(2,1)S(1)}, u32[]{:S(2)}, u32[]{:S(2)}) %collective-permute-start.8) | collective-permute-done | bytes 98336 | tf_op jit(solution)/shard_map/ppermute | solution.py:27
  76.1 1.9 %collective-permute-start.11 = (bf16[2,1,64,128]{3,2,1,0:T(8,128)(2,1)S(1)}, bf16[2,1,64,128]{3,2,1,0:T(8,128)(2,1)S(1)}, u32[]{:S(2)}, u32[]{:S(2)}) collective-permute-start(bf16[2,1,64,128]{3,2,1,0:T(8,128)(2,1)S(1)} %get-tuple-element.121), channel_id=1, source_target_pairs={{1,0},{2,1},{3,2},{5,4},{6,5},{7,6},{9,8},{10,9},{11,10},{13,12},{... | collective-permute-start | bytes 98312 | tf_op jit(solution)/shard_map/ppermute | solution.py:19
  78.0 2.4 %collective-permute-start.10 = (bf16[2,1,64,128]{3,2,1,0:T(8,128)(2,1)S(1)}, bf16[2,1,64,128]{3,2,1,0:T(8,128)(2,1)S(1)}, u32[]{:S(2)}, u32[]{:S(2)}) collective-permute-start(bf16[2,1,64,128]{3,2,1,0:T(8,128)(2,1)S(1)} %get-tuple-element.120), channel_id=1, source_target_pairs={{0,1},{1,2},{2,3},{4,5},{5,6},{6,7},{8,9},{9,10},{10,11},{12,13},{... | collective-permute-start | bytes 98312 | tf_op jit(solution)/shard_map/ppermute | solution.py:18
  80.4 0.7 convert_element_type.161
  81.1 2.1 %collective-permute-done.10 = bf16[2,1,64,128]{3,2,1,0:T(8,128)(2,1)S(1)} collective-permute-done((bf16[2,1,64,128]{3,2,1,0:T(8,128)(2,1)S(1)}, bf16[2,1,64,128]{3,2,1,0:T(8,128)(2,1)S(1)}, u32[]{:S(2)}, u32[]{:S(2)}) %collective-permute-start.10) | collective-permute-done | bytes 32800 | tf_op jit(solution)/shard_map/ppermute | solution.py:18
  85.0 1.9 %collective-permute-start.13 = (bf16[2,3,64,128]{3,2,1,0:T(8,128)(2,1)S(1)}, bf16[2,3,64,128]{3,2,1,0:T(8,128)(2,1)S(1)}, u32[]{:S(2)}, u32[]{:S(2)}) collective-permute-start(bf16[2,3,64,128]{3,2,1,0:T(8,128)(2,1)S(1)} %add_convert_fusion.2), channel_id=1, source_target_pairs={{4,0},{8,4},{12,8},{16,12},{20,16},{24,20},{28,24},{5,1},{9,5},{13... | collective-permute-start | bytes 294920 | tf_op jit(solution)/shard_map/ppermute | solution.py:19
  86.9 4.8 %collective-permute-start.12 = (bf16[2,3,64,128]{3,2,1,0:T(8,128)(2,1)S(1)}, bf16[2,3,64,128]{3,2,1,0:T(8,128)(2,1)S(1)}, u32[]{:S(2)}, u32[]{:S(2)}) collective-permute-start(bf16[2,3,64,128]{3,2,1,0:T(8,128)(2,1)S(1)} %add_convert_fusion.2), channel_id=1, source_target_pairs={{0,4},{4,8},{8,12},{12,16},{16,20},{20,24},{24,28},{1,5},{5,9},{9,... | collective-permute-start | bytes 294920 | tf_op jit(solution)/shard_map/ppermute | solution.py:18
  91.7 0.7 collective-permute-done.13
  92.4 1.5 %collective-permute-done.12 = bf16[2,3,64,128]{3,2,1,0:T(8,128)(2,1)S(1)} collective-permute-done((bf16[2,3,64,128]{3,2,1,0:T(8,128)(2,1)S(1)}, bf16[2,3,64,128]{3,2,1,0:T(8,128)(2,1)S(1)}, u32[]{:S(2)}, u32[]{:S(2)}) %collective-permute-start.12) | collective-permute-done | bytes 98336 | tf_op jit(solution)/shard_map/ppermute | solution.py:18
  94.0 0.6 gather_fusion.3
  94.9 0.6 fusion.3
  95.7 1.9 %collective-permute-start.15 = (bf16[8,1,64,256]{3,2,1,0:T(8,128)(2,1)S(1)}, bf16[8,1,64,256]{3,2,1,0:T(8,128)(2,1)S(1)}, u32[]{:S(2)}, u32[]{:S(2)}) collective-permute-start(bf16[8,1,64,256]{3,2,1,0:T(8,128)(2,1)S(1)} %get-tuple-element.88), channel_id=1, source_target_pairs={{1,0},{2,1},{3,2},{5,4},{6,5},{7,6},{9,8},{10,9},{11,10},{13,12},{... | collective-permute-start | bytes 786440 | tf_op jit(solution)/shard_map/ppermute | solution.py:19
  97.7 2.6 %collective-permute-start.14 = (bf16[8,1,64,256]{3,2,1,0:T(8,128)(2,1)S(1)}, bf16[8,1,64,256]{3,2,1,0:T(8,128)(2,1)S(1)}, u32[]{:S(2)}, u32[]{:S(2)}) collective-permute-start(bf16[8,1,64,256]{3,2,1,0:T(8,128)(2,1)S(1)} %get-tuple-element.87), channel_id=1, source_target_pairs={{0,1},{1,2},{2,3},{4,5},{5,6},{6,7},{8,9},{9,10},{10,11},{12,13},{... | collective-permute-start | bytes 786440 | tf_op jit(solution)/shard_map/ppermute | solution.py:18
  100.3 1.2 collective-permute-done.15
  101.5 3.8 %collective-permute-done.14 = bf16[8,1,64,256]{3,2,1,0:T(8,128)(2,1)S(1)} collective-permute-done((bf16[8,1,64,256]{3,2,1,0:T(8,128)(2,1)S(1)}, bf16[8,1,64,256]{3,2,1,0:T(8,128)(2,1)S(1)}, u32[]{:S(2)}, u32[]{:S(2)}) %collective-permute-start.14) | collective-permute-done | bytes 262176 | tf_op jit(solution)/shard_map/ppermute | solution.py:18
  105.4 0.9 select_maximum_fusion
  106.3 1.0 fusion.206
  110.5 0.4 fusion.10
  112.6 5.2 %collective-permute-start.17 = (bf16[2,24576]{1,0:T(2,128)(2,1)S(1)}, bf16[2,24576]{1,0:T(2,128)(2,1)S(1)}, u32[]{:S(2)}, u32[]{:S(2)}) collective-permute-start(bf16[2,24576]{1,0:T(2,128)(2,1)S(1)} %get-tuple-element.99), channel_id=1, source_target_pairs={{0,4},{4,8},{8,12},{12,16},{16,20},{20,24},{24,28},{1,5},{5,9},{9,... | collective-permute-start | bytes 294920 | tf_op jit(solution)/shard_map/ppermute | solution.py:27
  117.8 1.9 %collective-permute-start.16 = (bf16[2,24576]{1,0:T(2,128)(2,1)S(1)}, bf16[2,24576]{1,0:T(2,128)(2,1)S(1)}, u32[]{:S(2)}, u32[]{:S(2)}) collective-permute-start(bf16[2,24576]{1,0:T(2,128)(2,1)S(1)} %get-tuple-element.98), channel_id=1, source_target_pairs={{4,0},{8,4},{12,8},{16,12},{20,16},{24,20},{28,24},{5,1},{9,5},{13... | collective-permute-start | bytes 294920 | tf_op jit(solution)/shard_map/ppermute | solution.py:27
  119.8 0.7 collective-permute-done.17
  120.5 4.8 %collective-permute-done.16 = bf16[2,24576]{1,0:T(2,128)(2,1)S(1)} collective-permute-done((bf16[2,24576]{1,0:T(2,128)(2,1)S(1)}, bf16[2,24576]{1,0:T(2,128)(2,1)S(1)}, u32[]{:S(2)}, u32[]{:S(2)}) %collective-permute-start.16) | collective-permute-done | bytes 98336 | tf_op jit(solution)/shard_map/ppermute | solution.py:27
  125.5 1.9 %collective-permute-start.19 = (bf16[2,1,64,128]{3,2,1,0:T(8,128)(2,1)S(1)}, bf16[2,1,64,128]{3,2,1,0:T(8,128)(2,1)S(1)}, u32[]{:S(2)}, u32[]{:S(2)}) collective-permute-start(bf16[2,1,64,128]{3,2,1,0:T(8,128)(2,1)S(1)} %get-tuple-element.117), channel_id=1, source_target_pairs={{1,0},{2,1},{3,2},{5,4},{6,5},{7,6},{9,8},{10,9},{11,10},{13,12},{... | collective-permute-start | bytes 98312 | tf_op jit(solution)/shard_map/ppermute | solution.py:19
  127.4 2.4 %collective-permute-start.18 = (bf16[2,1,64,128]{3,2,1,0:T(8,128)(2,1)S(1)}, bf16[2,1,64,128]{3,2,1,0:T(8,128)(2,1)S(1)}, u32[]{:S(2)}, u32[]{:S(2)}) collective-permute-start(bf16[2,1,64,128]{3,2,1,0:T(8,128)(2,1)S(1)} %get-tuple-element.116), channel_id=1, source_target_pairs={{0,1},{1,2},{2,3},{4,5},{5,6},{6,7},{8,9},{9,10},{10,11},{12,13},{... | collective-permute-start | bytes 98312 | tf_op jit(solution)/shard_map/ppermute | solution.py:18
  129.9 2.7 %collective-permute-done.18 = bf16[2,1,64,128]{3,2,1,0:T(8,128)(2,1)S(1)} collective-permute-done((bf16[2,1,64,128]{3,2,1,0:T(8,128)(2,1)S(1)}, bf16[2,1,64,128]{3,2,1,0:T(8,128)(2,1)S(1)}, u32[]{:S(2)}, u32[]{:S(2)}) %collective-permute-start.18) | collective-permute-done | bytes 32800 | tf_op jit(solution)/shard_map/ppermute | solution.py:18
  134.4 0.7 add_convert_fusion.1
  (157 shorter events, 18.7 us)
Async XLA Ops:
  0.0 46.6 %copy-start = (bf16[256,256]{1,0:T(8,128)(2,1)S(1)}, bf16[256,256]{1,0:T(8,128)(2,1)}, u32[]{:S(2)}) copy-start(bf16[256,256]{1,0:T(8,128)(2,1)} %param.14) | copy-start | bytes 393220
  0.0 22.9 %copy-start.3 = (bf16[2,3,64,128]{3,2,1,0:T(8,128)(2,1)S(1)}, bf16[2,3,64,128]{3,2,1,0:T(8,128)(2,1)}, u32[]{:S(2)}) copy-start(bf16[2,3,64,128]{3,2,1,0:T(8,128)(2,1)} %param.11) | copy-start | bytes 294916
  0.0 22.9 %collective-permute-start.1 = (bf16[2,3,64,128]{3,2,1,0:T(8,128)(2,1)}, bf16[2,3,64,128]{3,2,1,0:T(8,128)(2,1)S(1)}, u32[]{:S(2)}, u32[]{:S(2)}) collective-permute-start(bf16[2,3,64,128]{3,2,1,0:T(8,128)(2,1)} %param.11), channel_id=1, source_target_pairs={{4,0},{8,4},{12,8},{16,12},{20,16},{24,20},{28,24},{5,1},{9,5},{13... | collective-permute-start | bytes 294920 | tf_op jit(solution)/shard_map/ppermute | solution.py:19
  2.6 20.3 %collective-permute-start = (bf16[2,3,64,128]{3,2,1,0:T(8,128)(2,1)}, bf16[2,3,64,128]{3,2,1,0:T(8,128)(2,1)S(1)}, u32[]{:S(2)}, u32[]{:S(2)}) collective-permute-start(bf16[2,3,64,128]{3,2,1,0:T(8,128)(2,1)} %param.11), channel_id=1, source_target_pairs={{0,4},{4,8},{8,12},{12,16},{16,20},{20,24},{24,28},{1,5},{5,9},{9,... | collective-permute-start | bytes 294920 | tf_op jit(solution)/shard_map/ppermute | solution.py:18
  6.9 9.2 %collective-permute-start.2 = (bf16[2,3,64,128]{3,2,1,0:T(8,128)(2,1)}, bf16[2,3,64,128]{3,2,1,0:T(8,128)(2,1)S(1)}, u32[]{:S(2)}, u32[]{:S(2)}) collective-permute-start(bf16[2,3,64,128]{3,2,1,0:T(8,128)(2,1)} %param.10), channel_id=1, source_target_pairs={{0,4},{4,8},{8,12},{12,16},{16,20},{20,24},{24,28},{1,5},{5,9},{9,... | collective-permute-start | bytes 294920 | tf_op jit(solution)/shard_map/ppermute | solution.py:18
  9.4 7.6 %collective-permute-start.3 = (bf16[2,3,64,128]{3,2,1,0:T(8,128)(2,1)}, bf16[2,3,64,128]{3,2,1,0:T(8,128)(2,1)S(1)}, u32[]{:S(2)}, u32[]{:S(2)}) collective-permute-start(bf16[2,3,64,128]{3,2,1,0:T(8,128)(2,1)} %param.10), channel_id=1, source_target_pairs={{4,0},{8,4},{12,8},{16,12},{20,16},{24,20},{28,24},{5,1},{9,5},{13... | collective-permute-start | bytes 294920 | tf_op jit(solution)/shard_map/ppermute | solution.py:19
  16.0 48.5 %copy-start.7 = (s32[8]{0:T(128)}, s32[8]{0:T(128)S(1)}, u32[]{:S(2)}) copy-start(s32[8]{0:T(128)S(1)} %get-tuple-element.124) | copy-start | bytes 100
  16.0 48.5 %copy-start.9 = (s32[8]{0:T(128)}, s32[8]{0:T(128)S(1)}, u32[]{:S(2)}) copy-start(s32[8]{0:T(128)S(1)} %get-tuple-element.125) | copy-start | bytes 100
  17.8 7.2 %collective-permute-start.5 = (bf16[8,3,64,128]{3,2,1,0:T(8,128)(2,1)S(1)}, bf16[8,3,64,128]{3,2,1,0:T(8,128)(2,1)S(1)}, u32[]{:S(2)}, u32[]{:S(2)}) collective-permute-start(bf16[8,3,64,128]{3,2,1,0:T(8,128)(2,1)S(1)} %broadcast_select_fusion), channel_id=1, source_target_pairs={{1,0},{2,1},{3,2},{5,4},{6,5},{7,6},{9,8},{10,9},{11,10},{13,12},{... | collective-permute-start | bytes 1179656 | tf_op jit(solution)/shard_map/ppermute | solution.py:19
  19.8 9.1 %collective-permute-start.4 = (bf16[8,3,64,128]{3,2,1,0:T(8,128)(2,1)S(1)}, bf16[8,3,64,128]{3,2,1,0:T(8,128)(2,1)S(1)}, u32[]{:S(2)}, u32[]{:S(2)}) collective-permute-start(bf16[8,3,64,128]{3,2,1,0:T(8,128)(2,1)S(1)} %broadcast_select_fusion), channel_id=1, source_target_pairs={{0,1},{1,2},{2,3},{4,5},{5,6},{6,7},{8,9},{9,10},{10,11},{12,13},{... | collective-permute-start | bytes 1179656 | tf_op jit(solution)/shard_map/ppermute | solution.py:18
  39.7 6.2 %copy-start.6 = (bf16[49,128]{1,0:T(8,128)(2,1)S(1)}, bf16[49,128]{1,0:T(8,128)(2,1)}, u32[]{:S(2)}) copy-start(bf16[49,128]{1,0:T(8,128)(2,1)} %param.13) | copy-start | bytes 37636
  47.5 5.8 %collective-permute-start.7 = (bf16[8,1,64,256]{3,2,1,0:T(8,128)(2,1)S(1)}, bf16[8,1,64,256]{3,2,1,0:T(8,128)(2,1)S(1)}, u32[]{:S(2)}, u32[]{:S(2)}) collective-permute-start(bf16[8,1,64,256]{3,2,1,0:T(8,128)(2,1)S(1)} %get-tuple-element.95), channel_id=1, source_target_pairs={{1,0},{2,1},{3,2},{5,4},{6,5},{7,6},{9,8},{10,9},{11,10},{13,12},{... | collective-permute-start | bytes 786440 | tf_op jit(solution)/shard_map/ppermute | solution.py:19
  49.4 7.7 %collective-permute-start.6 = (bf16[8,1,64,256]{3,2,1,0:T(8,128)(2,1)S(1)}, bf16[8,1,64,256]{3,2,1,0:T(8,128)(2,1)S(1)}, u32[]{:S(2)}, u32[]{:S(2)}) collective-permute-start(bf16[8,1,64,256]{3,2,1,0:T(8,128)(2,1)S(1)} %get-tuple-element.94), channel_id=1, source_target_pairs={{0,1},{1,2},{2,3},{4,5},{5,6},{6,7},{8,9},{9,10},{10,11},{12,13},{... | collective-permute-start | bytes 786440 | tf_op jit(solution)/shard_map/ppermute | solution.py:18
  58.0 1.1 copy-start.1
  62.7 0.8 copy-start.5
  64.8 18.6 %copy-start.2 = (bf16[9,128,128]{2,1,0:T(8,128)(2,1)S(1)}, bf16[9,128,128]{2,1,0:T(8,128)(2,1)}, u32[]{:S(2)}) copy-start(bf16[9,128,128]{2,1,0:T(8,128)(2,1)} %param.17) | copy-start | bytes 884740
  65.0 6.9 %collective-permute-start.9 = (bf16[2,24576]{1,0:T(2,128)(2,1)S(1)}, bf16[2,24576]{1,0:T(2,128)(2,1)S(1)}, u32[]{:S(2)}, u32[]{:S(2)}) collective-permute-start(bf16[2,24576]{1,0:T(2,128)(2,1)S(1)} %get-tuple-element.101), channel_id=1, source_target_pairs={{0,4},{4,8},{8,12},{12,16},{16,20},{20,24},{24,28},{1,5},{5,9},{9,... | collective-permute-start | bytes 294920 | tf_op jit(solution)/shard_map/ppermute | solution.py:27
  68.4 7.4 %collective-permute-start.8 = (bf16[2,24576]{1,0:T(2,128)(2,1)S(1)}, bf16[2,24576]{1,0:T(2,128)(2,1)S(1)}, u32[]{:S(2)}, u32[]{:S(2)}) collective-permute-start(bf16[2,24576]{1,0:T(2,128)(2,1)S(1)} %get-tuple-element.100), channel_id=1, source_target_pairs={{4,0},{8,4},{12,8},{16,12},{20,16},{24,20},{28,24},{5,1},{9,5},{13... | collective-permute-start | bytes 294920 | tf_op jit(solution)/shard_map/ppermute | solution.py:27
  76.1 5.1 %collective-permute-start.11 = (bf16[2,1,64,128]{3,2,1,0:T(8,128)(2,1)S(1)}, bf16[2,1,64,128]{3,2,1,0:T(8,128)(2,1)S(1)}, u32[]{:S(2)}, u32[]{:S(2)}) collective-permute-start(bf16[2,1,64,128]{3,2,1,0:T(8,128)(2,1)S(1)} %get-tuple-element.121), channel_id=1, source_target_pairs={{1,0},{2,1},{3,2},{5,4},{6,5},{7,6},{9,8},{10,9},{11,10},{13,12},{... | collective-permute-start | bytes 98312 | tf_op jit(solution)/shard_map/ppermute | solution.py:19
  78.0 5.2 %collective-permute-start.10 = (bf16[2,1,64,128]{3,2,1,0:T(8,128)(2,1)S(1)}, bf16[2,1,64,128]{3,2,1,0:T(8,128)(2,1)S(1)}, u32[]{:S(2)}, u32[]{:S(2)}) collective-permute-start(bf16[2,1,64,128]{3,2,1,0:T(8,128)(2,1)S(1)} %get-tuple-element.120), channel_id=1, source_target_pairs={{0,1},{1,2},{2,3},{4,5},{5,6},{6,7},{8,9},{9,10},{10,11},{12,13},{... | collective-permute-start | bytes 98312 | tf_op jit(solution)/shard_map/ppermute | solution.py:18
  83.4 0.9 copy-start.4
  85.0 7.4 %collective-permute-start.13 = (bf16[2,3,64,128]{3,2,1,0:T(8,128)(2,1)S(1)}, bf16[2,3,64,128]{3,2,1,0:T(8,128)(2,1)S(1)}, u32[]{:S(2)}, u32[]{:S(2)}) collective-permute-start(bf16[2,3,64,128]{3,2,1,0:T(8,128)(2,1)S(1)} %add_convert_fusion.2), channel_id=1, source_target_pairs={{4,0},{8,4},{12,8},{16,12},{20,16},{24,20},{28,24},{5,1},{9,5},{13... | collective-permute-start | bytes 294920 | tf_op jit(solution)/shard_map/ppermute | solution.py:19
  86.9 7.0 %collective-permute-start.12 = (bf16[2,3,64,128]{3,2,1,0:T(8,128)(2,1)S(1)}, bf16[2,3,64,128]{3,2,1,0:T(8,128)(2,1)S(1)}, u32[]{:S(2)}, u32[]{:S(2)}) collective-permute-start(bf16[2,3,64,128]{3,2,1,0:T(8,128)(2,1)S(1)} %add_convert_fusion.2), channel_id=1, source_target_pairs={{0,4},{4,8},{8,12},{12,16},{16,20},{20,24},{24,28},{1,5},{5,9},{9,... | collective-permute-start | bytes 294920 | tf_op jit(solution)/shard_map/ppermute | solution.py:18
  95.7 5.8 %collective-permute-start.15 = (bf16[8,1,64,256]{3,2,1,0:T(8,128)(2,1)S(1)}, bf16[8,1,64,256]{3,2,1,0:T(8,128)(2,1)S(1)}, u32[]{:S(2)}, u32[]{:S(2)}) collective-permute-start(bf16[8,1,64,256]{3,2,1,0:T(8,128)(2,1)S(1)} %get-tuple-element.88), channel_id=1, source_target_pairs={{1,0},{2,1},{3,2},{5,4},{6,5},{7,6},{9,8},{10,9},{11,10},{13,12},{... | collective-permute-start | bytes 786440 | tf_op jit(solution)/shard_map/ppermute | solution.py:19
  97.7 7.7 %collective-permute-start.14 = (bf16[8,1,64,256]{3,2,1,0:T(8,128)(2,1)S(1)}, bf16[8,1,64,256]{3,2,1,0:T(8,128)(2,1)S(1)}, u32[]{:S(2)}, u32[]{:S(2)}) collective-permute-start(bf16[8,1,64,256]{3,2,1,0:T(8,128)(2,1)S(1)} %get-tuple-element.87), channel_id=1, source_target_pairs={{0,1},{1,2},{2,3},{4,5},{5,6},{6,7},{8,9},{9,10},{10,11},{12,13},{... | collective-permute-start | bytes 786440 | tf_op jit(solution)/shard_map/ppermute | solution.py:18
  111.5 0.7 copy-start.8
  111.5 0.7 copy-start.10
  112.6 7.8 %collective-permute-start.17 = (bf16[2,24576]{1,0:T(2,128)(2,1)S(1)}, bf16[2,24576]{1,0:T(2,128)(2,1)S(1)}, u32[]{:S(2)}, u32[]{:S(2)}) collective-permute-start(bf16[2,24576]{1,0:T(2,128)(2,1)S(1)} %get-tuple-element.99), channel_id=1, source_target_pairs={{0,4},{4,8},{8,12},{12,16},{16,20},{20,24},{24,28},{1,5},{5,9},{9,... | collective-permute-start | bytes 294920 | tf_op jit(solution)/shard_map/ppermute | solution.py:27
  117.8 7.4 %collective-permute-start.16 = (bf16[2,24576]{1,0:T(2,128)(2,1)S(1)}, bf16[2,24576]{1,0:T(2,128)(2,1)S(1)}, u32[]{:S(2)}, u32[]{:S(2)}) collective-permute-start(bf16[2,24576]{1,0:T(2,128)(2,1)S(1)} %get-tuple-element.98), channel_id=1, source_target_pairs={{4,0},{8,4},{12,8},{16,12},{20,16},{24,20},{28,24},{5,1},{9,5},{13... | collective-permute-start | bytes 294920 | tf_op jit(solution)/shard_map/ppermute | solution.py:27
  125.5 4.4 %collective-permute-start.19 = (bf16[2,1,64,128]{3,2,1,0:T(8,128)(2,1)S(1)}, bf16[2,1,64,128]{3,2,1,0:T(8,128)(2,1)S(1)}, u32[]{:S(2)}, u32[]{:S(2)}) collective-permute-start(bf16[2,1,64,128]{3,2,1,0:T(8,128)(2,1)S(1)} %get-tuple-element.117), channel_id=1, source_target_pairs={{1,0},{2,1},{3,2},{5,4},{6,5},{7,6},{9,8},{10,9},{11,10},{13,12},{... | collective-permute-start | bytes 98312 | tf_op jit(solution)/shard_map/ppermute | solution.py:19
  127.4 5.2 %collective-permute-start.18 = (bf16[2,1,64,128]{3,2,1,0:T(8,128)(2,1)S(1)}, bf16[2,1,64,128]{3,2,1,0:T(8,128)(2,1)S(1)}, u32[]{:S(2)}, u32[]{:S(2)}) collective-permute-start(bf16[2,1,64,128]{3,2,1,0:T(8,128)(2,1)S(1)} %get-tuple-element.116), channel_id=1, source_target_pairs={{0,1},{1,2},{2,3},{4,5},{5,6},{6,7},{8,9},{9,10},{10,11},{12,13},{... | collective-permute-start | bytes 98312 | tf_op jit(solution)/shard_map/ppermute | solution.py:18
where the time goes:
time: 136 us; the launch traced here: 135 us
  starting transfers between devices  54.5 us (40%)
  waiting for transfers between devices  33 us (24%)
  other arithmetic  20.1 us (15%)
  local copies, waits for them, and re-layouts  13.6 us (10%)
  matrix products  13 us (10%)
    ppermute x8, starting transfers between devices, with_halo(): before = lax.ppermute(last, axis, up)  24.1 us
    ppermute x8, waiting for transfers between devices, with_halo(): before = lax.ppermute(last, axis, up)  17.8 us
    ppermute x8, starting transfers between devices, with_halo(): after = lax.ppermute(leading, axis, down)  17.4 us
    ppermute x4, starting transfers between devices, passed_along(): return lax.ppermute(block, axis, route)  13 us
    dot_general x4, other arithmetic, local(): jnp.einsum('syxc,syxc->syx', src_feat, moved, preferred_element_type=jnp....  11.5 us
    ppermute x4, waiting for transfers between devices, passed_along(): return lax.ppermute(block, axis, route)  10.4 us
    dot_general x36, matrix products, conv_taps(): jnp.dot(window, kernel[3 * row_off + col_off], preferred_element_type=jnp...  9.49 us
    another operation x50, local copies, waits for them, and re-layouts, local(): corr = (jnp.stack(columns, axis=-1) * scale).astype(jnp.bfloat16)  4.8 us
  transfers between devices with their start and end apart: 20, of which 15 were waited for; matrix products, arithmetic and copies ran while one was open for 5% of the time, Pallas kernels for 0%

commit v1 on v0

v1 whole, which is shorter than its diff:
```python
import functools

import jax
import jax.numpy as jnp
from jax import lax
from jax.experimental import pallas as pl
from jax.experimental.pallas import tpu as pltpu
from jax.sharding import PartitionSpec as P

RADIUS = 3
ROUNDS = 2
CAPACITY = 8
LANES = 128
MESH = pl.DeviceIdType.MESH
F32 = jnp.float32
BF16 = jnp.bfloat16
LEFT, RIGHT, UP, DOWN = range(4)


def dot(a, b):
    return jnp.dot(a, b, preferred_element_type=F32)


def dot_nt(a, b):
    return lax.dot_general(a, b, (((1,), (1,)), ((), ())), preferred_element_type=F32)


def kernel(
    nf, nr,
    pairs_ref, fmap_ref, ctx_ref, wcorr_ref, wzr_ref, wq_ref, wmsg_ref, wres_ref,
    out_ref,
    fwin, cwin, motion, hid, zbuf, qr, qx, msend, mrecv, mown, ubuf, sbuf,
    wsel, wq_s, wres_s, wmsg_s, tbl,
    ssem, rsem, lsem,
):
    f = lax.axis_index("frames")
    r = lax.axis_index("rows")
    fd, height, width, chans = fmap_ref.shape
    npair = pairs_ref.shape[0]
    rows = height * width
    has = {LEFT: f > 0, RIGHT: f < nf - 1, UP: r > 0, DOWN: r < nr - 1}
    dev = {LEFT: (f - 1, r), RIGHT: (f + 1, r), UP: (f, r - 1), DOWN: (f, r + 1)}
    back = {LEFT: RIGHT, RIGHT: LEFT, UP: DOWN, DOWN: UP}
    sent = []

    def rcopy(i, way, src, dst):
        return pltpu.make_async_remote_copy(
            src_ref=src, dst_ref=dst, send_sem=ssem.at[i], recv_sem=rsem.at[i],
            device_id=dev[way], device_id_type=MESH,
        )

    def push(i, way, src, dst, cond=None):
        cond = has[way] if cond is None else jnp.logical_and(cond, has[way])
        sent.append((i, way, src, dst, cond))

        @pl.when(cond)
        def _():
            rcopy(i, way, src, dst).start()

    def arrive(i, way, src, dst, cond=None):
        cond = has[back[way]] if cond is None else jnp.logical_and(cond, has[back[way]])

        @pl.when(cond)
        def _():
            rcopy(i, way, src, dst).wait_recv()

    own_rows = pl.ds(RADIUS, height)
    place = {RIGHT: pl.ds(0, fd), LEFT: pl.ds(2 * fd, fd)}
    middle = pl.ds(fd, fd)

    own_f = pltpu.make_async_copy(fmap_ref, fwin.at[middle, own_rows], lsem.at[0])
    own_c = pltpu.make_async_copy(ctx_ref, cwin.at[0, middle], lsem.at[1])
    own_f.start()
    own_c.start()

    barrier = pltpu.get_barrier_semaphore()
    count = 0
    for way in (LEFT, RIGHT, UP, DOWN):
        count = count + has[way].astype(jnp.int32)

        @pl.when(has[way])
        def _(way=way):
            pl.semaphore_signal(barrier, inc=1, device_id=dev[way], device_id_type=MESH)

    pl.semaphore_wait(barrier, count)

    for way in (RIGHT, LEFT):
        push(way, way, fmap_ref, fwin.at[place[way], own_rows])
    edge_src = {UP: pl.ds(RADIUS, RADIUS), DOWN: pl.ds(height, RADIUS)}
    edge_dst = {UP: pl.ds(RADIUS + height, RADIUS), DOWN: pl.ds(0, RADIUS)}
    feat_edge = {UP: pl.ds(0, RADIUS), DOWN: pl.ds(height - RADIUS, RADIUS)}
    for way in (UP, DOWN):
        push(way, way, fmap_ref.at[:, feat_edge[way]], fwin.at[middle, edge_dst[way]])
    for way in (RIGHT, LEFT):
        push(4 + way, way, ctx_ref, cwin.at[0, place[way]])

    fwin[:, 2 * RADIUS + height] = jnp.zeros(
        (fwin.shape[0],) + fwin.shape[2:], BF16
    )

    @pl.when(r == 0)
    def _():
        fwin[:, 0:RADIUS] = jnp.zeros((fwin.shape[0], RADIUS, width, chans), BF16)
        for k in range(ROUNDS):
            qr[k, :, 0] = jnp.zeros((CAPACITY, width, chans), BF16)
            qx[k, :, 0] = jnp.zeros((CAPACITY, width, chans), BF16)
            ubuf[k, :, 0] = jnp.zeros((fd, width, chans), BF16)

    @pl.when(r == nr - 1)
    def _():
        fwin[:, RADIUS + height : 2 * RADIUS + height] = jnp.zeros(
            (fwin.shape[0], RADIUS, width, chans), BF16
        )
        for k in range(ROUNDS):
            qr[k, :, height + 1] = jnp.zeros((CAPACITY, width, chans), BF16)
            qx[k, :, height + 1] = jnp.zeros((CAPACITY, width, chans), BF16)
            ubuf[k, :, height + 1] = jnp.zeros((fd, width, chans), BF16)

    for way, edge in ((RIGHT, f == 0), (LEFT, f == nf - 1)):
        @pl.when(edge)
        def _(way=way):
            fwin[place[way]] = jnp.zeros((fd,) + fwin.shape[1:], BF16)
            for k in range(ROUNDS):
                cwin[k, place[way]] = jnp.zeros((fd, height, width, chans), BF16)
                mrecv[k, way] = jnp.zeros((fd, rows, chans), BF16)

    zero = jnp.int32(0)

    def pick(p, carry):
        seen, srcs, tgts, ok = carry
        mine = (pairs_ref[p, 2] == f).astype(jnp.int32)
        s, t = pairs_ref[p, 0], pairs_ref[p, 1]
        hits = [mine * (seen == k).astype(jnp.int32) for k in range(CAPACITY)]
        srcs = tuple(v + h * s for v, h in zip(srcs, hits))
        tgts = tuple(v + h * t for v, h in zip(tgts, hits))
        ok = tuple(v + h for v, h in zip(ok, hits))
        return seen + mine, srcs, tgts, ok

    zeros = (zero,) * CAPACITY
    _, srcs, tgts, oks = lax.fori_loop(0, npair, pick, (zero, zeros, zeros, zeros))
    first = (f - 1) * fd
    last = 3 * fd - 1
    for k in range(CAPACITY):
        s_idx = jnp.clip(srcs[k] - first, 0, last)
        t_idx = jnp.clip(tgts[k] - first, 0, last)
        tbl[0, k] = s_idx
        tbl[1, k] = t_idx
        tbl[2, k] = jnp.where(oks[k] == 1, s_idx, -1)
        tbl[3, k] = jnp.where(oks[k] == 1, t_idx, -1)

    span = 2 * RADIUS + 1
    per = LANES // width
    groups = (span + per - 1) // per
    depth = groups * LANES
    line = lax.broadcasted_iota(jnp.int32, (depth, wcorr_ref.shape[0]), 0)
    col = lax.broadcasted_iota(jnp.int32, (depth, wcorr_ref.shape[0]), 1)
    lane = lax.rem(line, LANES) + RADIUS + 1
    b_off = lax.rem(lane, width)
    a_off = lax.div(line, LANES) * per + lax.rem(lax.div(lane, width) + per - 1, per)
    take = jnp.logical_and(b_off < span, a_off < span)
    index = jnp.where(take, a_off * span + b_off, -1)
    wsel[...] = dot(
        jnp.where(index == col, 1.0, 0.0).astype(BF16), wcorr_ref[...]
    ).astype(BF16)
    for k in range(3):
        for j in range(3):
            wq_s[k, :, j * chans : (j + 1) * chans] = wq_ref[3 * k + j]
            wres_s[k, :, j * chans : (j + 1) * chans] = wres_ref[3 * k + j]
    wmsg_s[0:chans] = wmsg_ref[:, 0:chans]
    wmsg_s[chans : 2 * chans] = wmsg_ref[:, chans : 2 * chans]

    own_f.wait()
    for way in (RIGHT, LEFT):
        arrive(way, way, fmap_ref, fwin.at[place[way], own_rows])
        for n, side in enumerate((UP, DOWN)):
            push(
                8 + 2 * way + n, side, fwin.at[place[way], edge_src[side]],
                fwin.at[place[way], edge_dst[side]], cond=has[back[way]],
            )
    for side in (UP, DOWN):
        arrive(side, side, fmap_ref.at[:, feat_edge[side]], fwin.at[middle, edge_dst[side]])
    for way in (RIGHT, LEFT):
        for n, side in enumerate((UP, DOWN)):
            arrive(
                8 + 2 * way + n, side, fwin.at[place[way], edge_src[side]],
                fwin.at[place[way], edge_dst[side]], cond=has[back[way]],
            )

    xs = width - 1 - lax.broadcasted_iota(jnp.int32, (width, LANES), 0)
    ls = lax.broadcasted_iota(jnp.int32, (width, LANES), 1) + RADIUS + 1
    bs = lax.rem(ls, width)
    flip = jnp.where(
        lax.broadcasted_iota(jnp.int32, (width, width), 0)
        + lax.broadcasted_iota(jnp.int32, (width, width), 1)
        == width - 1,
        1.0,
        0.0,
    ).astype(BF16)
    inside = jnp.logical_and(xs + bs >= RADIUS, xs + bs < width + RADIUS)
    inside = jnp.logical_and(inside, bs < span)
    scale = 1.0 / chans**0.5

    @pl.loop(0, CAPACITY)
    def _(s):
        src_i, tgt_i = tbl[0, s], tbl[1, s]
        lines = []
        for y in range(height):
            a = dot(flip, fwin[src_i, RADIUS + y]).astype(BF16)
            b = fwin[tgt_i, pl.ds(y, groups * per)].reshape(groups * per * width, chans)
            g = dot_nt(a, b) * scale
            tiles = []
            for j in range(groups):
                tile = pltpu.roll(
                    g[:, j * LANES : (j + 1) * LANES], 0, 1, stride=1, stride_axis=0
                )
                tiles.append(jnp.where(inside, tile, 0.0).astype(BF16))
            lines.append(jnp.concatenate(tiles, axis=1))
        corr = jnp.concatenate(lines, axis=0)
        moved = jnp.maximum(dot(corr, wsel[...]), 0.0).astype(BF16)
        for y in range(height):
            motion[s, y * width : (y + 1) * width] = dot(
                flip, moved[y * width : (y + 1) * width]
            ).astype(BF16)

    own_c.wait()
    for way in (RIGHT, LEFT):
        arrive(4 + way, way, ctx_ref, cwin.at[0, place[way]])

    line_no = lax.rem(lax.broadcasted_iota(jnp.int32, (rows, chans), 0), width)
    not_first = line_no > 0
    not_last = line_no < width - 1

    def shifted_sum(acc):
        before = pltpu.roll(acc[:, 0:chans], 1, 0)
        after = pltpu.roll(acc[:, 2 * chans : 3 * chans], rows - 1, 0)
        return (
            jnp.where(not_first, before, 0.0)
            + acc[:, chans : 2 * chans]
            + jnp.where(not_last, after, 0.0)
        )

    halo_src = {UP: 1, DOWN: height}
    halo_dst = {UP: height + 1, DOWN: 0}

    for k in range(ROUNDS):
        base = 16 + 16 * k

        @pl.loop(0, CAPACITY)
        def _(s):
            state = cwin[k, tbl[0, s]].reshape(rows, chans).astype(F32)
            if k == 0:
                hid[s] = jnp.tanh(state)
            xin = (motion[s].astype(F32) + state).astype(BF16)
            qx[k, s, pl.ds(1, height)] = xin.reshape(height, width, chans)

        for n, side in enumerate((UP, DOWN)):
            push(base + n, side, qx.at[k, :, halo_src[side]], qx.at[k, :, halo_dst[side]])

        @pl.loop(0, CAPACITY)
        def _(s):
            h = hid[s]
            xin = qx[k, s, pl.ds(1, height)].reshape(rows, chans)
            gates = jax.nn.sigmoid(dot(jnp.concatenate([h.astype(BF16), xin], axis=1), wzr_ref[...]))
            zbuf[s] = gates[:, 0:chans]
            qr[k, s, pl.ds(1, height)] = (
                (gates[:, chans : 2 * chans] * h).astype(BF16).reshape(height, width, chans)
            )

        for n, side in enumerate((UP, DOWN)):
            push(base + 2 + n, side, qr.at[k, :, halo_src[side]], qr.at[k, :, halo_dst[side]])
        for n, side in enumerate((UP, DOWN)):
            arrive(base + n, side, qx.at[k, :, halo_src[side]], qx.at[k, :, halo_dst[side]])
            arrive(base + 2 + n, side, qr.at[k, :, halo_src[side]], qr.at[k, :, halo_dst[side]])

        @pl.loop(0, CAPACITY)
        def _(s):
            acc = None
            for dy in range(3):
                part = jnp.concatenate(
                    [
                        qr[k, s, pl.ds(dy, height)].reshape(rows, chans),
                        qx[k, s, pl.ds(dy, height)].reshape(rows, chans),
                    ],
                    axis=1,
                )
                term = dot(part, wq_s[dy])
                acc = term if acc is None else acc + term
            cand = jnp.tanh(shifted_sum(acc))
            z = zbuf[s]
            hid[s] = (1.0 - z) * hid[s] + z * cand

        def message(j):
            first_sum = jnp.zeros((rows, chans), F32)
            second_sum = jnp.zeros((rows, chans), F32)
            for s in range(CAPACITY):
                h = hid[s]
                first_sum = first_sum + jnp.where(tbl[2, s] == j, 1.0, 0.0) * h
                second_sum = second_sum + jnp.where(tbl[3, s] == j, 1.0, 0.0) * h
            both = jnp.concatenate([first_sum.astype(BF16), second_sum.astype(BF16)], axis=1)
            return dot(both, wmsg_s[...])

        for way, start in ((LEFT, 0), (RIGHT, 2 * fd)):
            @pl.loop(0, fd)
            def _(j, way=way, start=start):
                msend[k, way, j] = message(start + j).astype(BF16)

            push(base + 4 + way, way, msend.at[k, way], mrecv.at[k, way])

        @pl.loop(0, fd)
        def _(j):
            mown[j] = message(fd + j)

        for way in (LEFT, RIGHT):
            arrive(base + 4 + way, way, msend.at[k, way], mrecv.at[k, way])

        @pl.loop(0, fd)
        def _(j):
            total = mown[j] + mrecv[k, LEFT, j].astype(F32) + mrecv[k, RIGHT, j].astype(F32)
            ubuf[k, j, pl.ds(1, height)] = (
                jnp.maximum(total, 0.0).astype(BF16).reshape(height, width, chans)
            )

        for n, side in enumerate((UP, DOWN)):
            push(base + 8 + n, side, ubuf.at[k, :, halo_src[side]], ubuf.at[k, :, halo_dst[side]])
        for n, side in enumerate((UP, DOWN)):
            arrive(base + 8 + n, side, ubuf.at[k, :, halo_src[side]], ubuf.at[k, :, halo_dst[side]])

        @pl.loop(0, fd)
        def _(j):
            acc = None
            for dy in range(3):
                term = dot(ubuf[k, j, pl.ds(dy, height)].reshape(rows, chans), wres_s[dy])
                acc = term if acc is None else acc + term
            old = cwin[k, fd + j].reshape(rows, chans).astype(F32)
            new = (old + shifted_sum(acc)).astype(BF16).reshape(height, width, chans)
            if k == ROUNDS - 1:
                out_ref[j] = new
            else:
                sbuf[k, j] = new
                cwin[k + 1, fd + j] = new

        if k < ROUNDS - 1:
            for way in (RIGHT, LEFT):
                push(base + 12 + way, way, sbuf.at[k], cwin.at[k + 1, place[way]])
            for way in (RIGHT, LEFT):
                arrive(base + 12 + way, way, sbuf.at[k], cwin.at[k + 1, place[way]])

    for i, way, src, dst, cond in sent:
        @pl.when(cond)
        def _(i=i, way=way, src=src, dst=dst):
            rcopy(i, way, src, dst).wait_send()


def local(nf, nr, fmap, context, pairs, w_corr, w_zr, w_q, w_msg, w_res):
    fd, height, width, chans = fmap.shape
    rows = height * width
    win = 3 * fd
    groups = -(-(2 * RADIUS + 1) // (LANES // width))
    vmem = pl.BlockSpec(memory_space=pltpu.VMEM)
    return pl.pallas_call(
        functools.partial(kernel, nf, nr),
        out_shape=jax.ShapeDtypeStruct(fmap.shape, BF16),
        in_specs=[pl.BlockSpec(memory_space=pltpu.SMEM)] + [vmem] * 7,
        out_specs=vmem,
        scratch_shapes=[
            pltpu.VMEM((win, 2 * RADIUS + height + 1, width, chans), BF16),
            pltpu.VMEM((ROUNDS, win, height, width, chans), BF16),
            pltpu.VMEM((CAPACITY, rows, chans), BF16),
            pltpu.VMEM((CAPACITY, rows, chans), F32),
            pltpu.VMEM((CAPACITY, rows, chans), F32),
            pltpu.VMEM((ROUNDS, CAPACITY, height + 2, width, chans), BF16),
            pltpu.VMEM((ROUNDS, CAPACITY, height + 2, width, chans), BF16),
            pltpu.VMEM((ROUNDS, 2, fd, rows, chans), BF16),
            pltpu.VMEM((ROUNDS, 2, fd, rows, chans), BF16),
            pltpu.VMEM((fd, rows, chans), F32),
            pltpu.VMEM((ROUNDS, fd, height + 2, width, chans), BF16),
            pltpu.VMEM((ROUNDS, fd, height, width, chans), BF16),
            pltpu.VMEM((groups * LANES, chans), BF16),
            pltpu.VMEM((3, 2 * chans, 3 * chans), BF16),
            pltpu.VMEM((3, chans, 3 * chans), BF16),
            pltpu.VMEM((2 * chans, chans), BF16),
            pltpu.SMEM((4, CAPACITY), jnp.int32),
            pltpu.SemaphoreType.DMA((16 + 16 * ROUNDS,)),
            pltpu.SemaphoreType.DMA((16 + 16 * ROUNDS,)),
            pltpu.SemaphoreType.DMA((2,)),
        ],
        compiler_params=pltpu.CompilerParams(collective_id=0, has_side_effects=True),
    )(pairs, fmap, context, w_corr, w_zr, w_q, w_msg, w_res)


def solution(mesh):
    placed = (P("frames", "rows", None, None), P("frames", "rows", None, None)) + (P(),) * 6
    return jax.shard_map(
        functools.partial(local, mesh.shape["frames"], mesh.shape["rows"]),
        mesh=mesh,
        in_specs=placed,
        out_specs=P("frames", "rows", None, None),
        check_vma=False,
    )
```

time: 136 us -> 64.8 us (0.48)
  the two profiles are of different devices: /device:TPU:14 before, /device:TPU:9 now
where the time goes in v1:
time: 64.8 us; the launch traced here: 64.6 us
  Pallas kernels  61.7 us (95%)
  local copies, waits for them, and re-layouts  2.91 us (4%)
    pallas_call x1, Pallas kernels, local(): pl.pallas_call(functools.partial(kernel, nf, nr), out_shape=jax.ShapeDtyp...  61.7 us
    unnamed x2, local copies, waits for them, and re-layouts  2.91 us

profile of v1, /device:TPU:9, one launch (start us, length us, event | category | flops | bytes accessed | tf_op | source)
XLA Modules:
  0.0 64.6 jit_solution(13751116574197484380)
XLA Ops:
  0.0 1.4 %copy.9.pairs_ref = s32[32,3]{1,0:T(8,128)} copy(s32[32,3]{0,1:T(4,128)} %param.10) | data formatting | bytes 768 | tf_op args[2]
  1.4 61.7 %shard_map.82 = bf16[2,3,64,128]{3,2,1,0:T(8,128)(2,1)} custom-call(s32[32,3]{1,0:T(8,128)} %copy.9.pairs_ref, bf16[2,3,64,128]{3,2,1,0:T(8,128)(2,1)} %fmap_ref.1, bf16[2,3,64,128]{3,2,1,0:T(8,128)(2,1)} %ctx_ref.1, bf16[49,128]{1,0:T(8,128)(2,1)} %wcorr_ref.1, bf16[256,256]{1,0:T(8,128)(2,1)} %wzr_ref.1, bf16[9,256,128]{2,1,0:T(8,128)(2,1)} %wq_ref.1, ...), custom_call_target="tpu_custom_call" | custom-call | tf_op jit(solution)/shard_map/pallas_call | solution.py:360
  63.1 1.5 %copy.11 = bf16[2,3,64,128]{3,2,1,0:T(8,128)(2,1)} copy(bf16[2,3,64,128]{3,2,1,0:T(8,128)(2,1)} %shard_map.82) | data formatting | bytes 196608

commit v2 on v1

--- a/solution.py
+++ b/solution.py
@@ -30,7 +30,7 @@
     pairs_ref, fmap_ref, ctx_ref, wcorr_ref, wzr_ref, wq_ref, wmsg_ref, wres_ref,
     out_ref,
     fwin, cwin, motion, hid, zbuf, qr, qx, msend, mrecv, mown, ubuf, sbuf,
-    wsel, wq_s, wres_s, wmsg_s, tbl,
+    wsel, wq_s, wres_s, wmsg_s, pre, rim, tbl,
     ssem, rsem, lsem,
 ):
     f = lax.axis_index("frames")
@@ -43,26 +43,30 @@
     back = {LEFT: RIGHT, RIGHT: LEFT, UP: DOWN, DOWN: UP}
     sent = []
 
-    def rcopy(i, way, src, dst):
+    def both(cond, gate):
+        return cond if gate is None else jnp.logical_and(cond, gate)
+
+    def rcopy(handle):
+        i, way, src, dst, _ = handle
         return pltpu.make_async_remote_copy(
             src_ref=src, dst_ref=dst, send_sem=ssem.at[i], recv_sem=rsem.at[i],
             device_id=dev[way], device_id_type=MESH,
         )
 
-    def push(i, way, src, dst, cond=None):
-        cond = has[way] if cond is None else jnp.logical_and(cond, has[way])
-        sent.append((i, way, src, dst, cond))
-
-        @pl.when(cond)
+    def push(way, src, dst, gate=None):
+        handle = (len(sent), way, src, dst, gate)
+        sent.append(handle)
+
+        @pl.when(both(has[way], gate))
         def _():
-            rcopy(i, way, src, dst).start()
-
-    def arrive(i, way, src, dst, cond=None):
-        cond = has[back[way]] if cond is None else jnp.logical_and(cond, has[back[way]])
-
-        @pl.when(cond)
+            rcopy(handle).start()
+
+        return handle
+
+    def arrive(handle):
+        @pl.when(both(has[back[handle[1]]], handle[4]))
         def _():
-            rcopy(i, way, src, dst).wait_recv()
+            rcopy(handle).wait_recv()
 
     own_rows = pl.ds(RADIUS, height)
     place = {RIGHT: pl.ds(0, fd), LEFT: pl.ds(2 * fd, fd)}
@@ -70,8 +74,15 @@
 
     own_f = pltpu.make_async_copy(fmap_ref, fwin.at[middle, own_rows], lsem.at[0])
     own_c = pltpu.make_async_copy(ctx_ref, cwin.at[0, middle], lsem.at[1])
-    own_f.start()
-    own_c.start()
+    loads = []
+    for k in range(3):
+        for j in range(3):
+            lanes = pl.ds(j * chans, chans)
+            loads.append((wq_ref.at[3 * k + j], wq_s.at[k, :, lanes]))
+            loads.append((wres_ref.at[3 * k + j], wres_s.at[k, :, lanes]))
+    loads = [
+        pltpu.make_async_copy(src, dst, lsem.at[2 + n]) for n, (src, dst) in enumerate(loads)
+    ]
 
     barrier = pltpu.get_barrier_semaphore()
     count = 0
@@ -82,17 +93,25 @@
         def _(way=way):
             pl.semaphore_signal(barrier, inc=1, device_id=dev[way], device_id_type=MESH)
 
+    own_f.start()
+    own_c.start()
+    for load in loads:
+        load.start()
     pl.semaphore_wait(barrier, count)
 
-    for way in (RIGHT, LEFT):
-        push(way, way, fmap_ref, fwin.at[place[way], own_rows])
+    seat = {RIGHT: 0, LEFT: 2 * fd}
+    feats = {}
+    for j in range(fd):
+        for way in (RIGHT, LEFT):
+            feats[way, j] = push(way, fmap_ref.at[j], fwin.at[seat[way] + j, own_rows])
     edge_src = {UP: pl.ds(RADIUS, RADIUS), DOWN: pl.ds(height, RADIUS)}
     edge_dst = {UP: pl.ds(RADIUS + height, RADIUS), DOWN: pl.ds(0, RADIUS)}
     feat_edge = {UP: pl.ds(0, RADIUS), DOWN: pl.ds(height - RADIUS, RADIUS)}
-    for way in (UP, DOWN):
-        push(way, way, fmap_ref.at[:, feat_edge[way]], fwin.at[middle, edge_dst[way]])
-    for way in (RIGHT, LEFT):
-        push(4 + way, way, ctx_ref, cwin.at[0, place[way]])
+    edges = [
+        push(way, fmap_ref.at[:, feat_edge[way]], fwin.at[middle, edge_dst[way]])
+        for way in (UP, DOWN)
+    ]
+    states = [push(way, ctx_ref, cwin.at[0, place[way]]) for way in (RIGHT, LEFT)]
 
     fwin[:, 2 * RADIUS + height] = jnp.zeros(
         (fwin.shape[0],) + fwin.shape[2:], BF16
@@ -162,29 +181,23 @@
     wsel[...] = dot(
         jnp.where(index == col, 1.0, 0.0).astype(BF16), wcorr_ref[...]
     ).astype(BF16)
-    for k in range(3):
-        for j in range(3):
-            wq_s[k, :, j * chans : (j + 1) * chans] = wq_ref[3 * k + j]
-            wres_s[k, :, j * chans : (j + 1) * chans] = wres_ref[3 * k + j]
     wmsg_s[0:chans] = wmsg_ref[:, 0:chans]
     wmsg_s[chans : 2 * chans] = wmsg_ref[:, chans : 2 * chans]
 
     own_f.wait()
-    for way in (RIGHT, LEFT):
-        arrive(way, way, fmap_ref, fwin.at[place[way], own_rows])
-        for n, side in enumerate((UP, DOWN)):
-            push(
-                8 + 2 * way + n, side, fwin.at[place[way], edge_src[side]],
-                fwin.at[place[way], edge_dst[side]], cond=has[back[way]],
-            )
-    for side in (UP, DOWN):
-        arrive(side, side, fmap_ref.at[:, feat_edge[side]], fwin.at[middle, edge_dst[side]])
-    for way in (RIGHT, LEFT):
-        for n, side in enumerate((UP, DOWN)):
-            arrive(
-                8 + 2 * way + n, side, fwin.at[place[way], edge_src[side]],
-                fwin.at[place[way], edge_dst[side]], cond=has[back[way]],
-            )
+    for j in range(fd):
+        for way in (RIGHT, LEFT):
+            arrive(feats[way, j])
+            spot = seat[way] + j
+            for side in (UP, DOWN):
+                edges.append(
+                    push(
+                        side, fwin.at[spot, edge_src[side]], fwin.at[spot, edge_dst[side]],
+                        gate=has[back[way]],
+                    )
+                )
+    for handle in edges:
+        arrive(handle)
 
     xs = width - 1 - lax.broadcasted_iota(jnp.int32, (width, LANES), 0)
     ls = lax.broadcasted_iota(jnp.int32, (width, LANES), 1) + RADIUS + 1
@@ -200,7 +213,7 @@
     inside = jnp.logical_and(inside, bs < span)
     scale = 1.0 / chans**0.5
 
-    @pl.loop(0, CAPACITY)
+    @pl.loop(0, CAPACITY, unroll=4)
     def _(s):
         src_i, tgt_i = tbl[0, s], tbl[1, s]
         lines = []
@@ -223,14 +236,14 @@
             ).astype(BF16)
 
     own_c.wait()
-    for way in (RIGHT, LEFT):
-        arrive(4 + way, way, ctx_ref, cwin.at[0, place[way]])
-
-    line_no = lax.rem(lax.broadcasted_iota(jnp.int32, (rows, chans), 0), width)
-    not_first = line_no > 0
-    not_last = line_no < width - 1
+    for load in loads:
+        load.wait()
 
     def shifted_sum(acc):
+        rows = acc.shape[0]
+        line_no = lax.rem(lax.broadcasted_iota(jnp.int32, (rows, chans), 0), width)
+        not_first = line_no > 0
+        not_last = line_no < width - 1
         before = pltpu.roll(acc[:, 0:chans], 1, 0)
         after = pltpu.roll(acc[:, 2 * chans : 3 * chans], rows - 1, 0)
         return (
@@ -239,13 +252,22 @@
             + jnp.where(not_last, after, 0.0)
         )
 
+    def conv_own(part, weight):
+        blank = jnp.zeros((width, 3 * chans), F32)
+        acc = dot(part, weight[1])
+        if height > 1:
+            acc = acc + jnp.concatenate([blank, dot(part[: rows - width], weight[0])], axis=0)
+            acc = acc + jnp.concatenate([dot(part[width:], weight[2]), blank], axis=0)
+        return shifted_sum(acc)
+
     halo_src = {UP: 1, DOWN: height}
     halo_dst = {UP: height + 1, DOWN: 0}
 
     for k in range(ROUNDS):
-        base = 16 + 16 * k
-
-        @pl.loop(0, CAPACITY)
+        for handle in states:
+            arrive(handle)
+
+        @pl.loop(0, CAPACITY, unroll=4)
         def _(s):
             state = cwin[k, tbl[0, s]].reshape(rows, chans).astype(F32)
             if k == 0:
@@ -253,10 +275,12 @@
             xin = (motion[s].astype(F32) + state).astype(BF16)
             qx[k, s, pl.ds(1, height)] = xin.reshape(height, width, chans)
 
-        for n, side in enumerate((UP, DOWN)):
-            push(base + n, side, qx.at[k, :, halo_src[side]], qx.at[k, :, halo_dst[side]])
-
-        @pl.loop(0, CAPACITY)
+        halos = [
+            push(side, qx.at[k, :, halo_src[side]], qx.at[k, :, halo_dst[side]])
+            for side in (UP, DOWN)
+        ]
+
+        @pl.loop(0, CAPACITY, unroll=4)
         def _(s):
             h = hid[s]
             xin = qx[k, s, pl.ds(1, height)].reshape(rows, chans)
@@ -266,28 +290,45 @@
                 (gates[:, chans : 2 * chans] * h).astype(BF16).reshape(height, width, chans)
             )
 
-        for n, side in enumerate((UP, DOWN)):
-            push(base + 2 + n, side, qr.at[k, :, halo_src[side]], qr.at[k, :, halo_dst[side]])
-        for n, side in enumerate((UP, DOWN)):
-            arrive(base + n, side, qx.at[k, :, halo_src[side]], qx.at[k, :, halo_dst[side]])
-            arrive(base + 2 + n, side, qr.at[k, :, halo_src[side]], qr.at[k, :, halo_dst[side]])
-
-        @pl.loop(0, CAPACITY)
+        halos += [
+            push(side, qr.at[k, :, halo_src[side]], qr.at[k, :, halo_dst[side]])
+            for side in (UP, DOWN)
+        ]
+
+        @pl.loop(0, CAPACITY, unroll=4)
         def _(s):
-            acc = None
-            for dy in range(3):
-                part = jnp.concatenate(
-                    [
-                        qr[k, s, pl.ds(dy, height)].reshape(rows, chans),
-                        qx[k, s, pl.ds(dy, height)].reshape(rows, chans),
-                    ],
-                    axis=1,
-                )
-                term = dot(part, wq_s[dy])
-                acc = term if acc is None else acc + term
-            cand = jnp.tanh(shifted_sum(acc))
-            z = zbuf[s]
-            hid[s] = (1.0 - z) * hid[s] + z * cand
+            part = jnp.concatenate(
+                [
+                    qr[k, s, pl.ds(1, height)].reshape(rows, chans),
+                    qx[k, s, pl.ds(1, height)].reshape(rows, chans),
+                ],
+                axis=1,
+            )
+            pre[s] = conv_own(part, wq_s)
+
+        for handle in halos:
+            arrive(handle)
+        for n, (line_at, tap) in enumerate(((0, 0), (height + 1, 2))):
+            part = jnp.concatenate(
+                [
+                    qr[k, :, line_at].reshape(CAPACITY * width, chans),
+                    qx[k, :, line_at].reshape(CAPACITY * width, chans),
+                ],
+                axis=1,
+            )
+            rim[n] = shifted_sum(dot(part, wq_s[tap])).reshape(CAPACITY, width, chans)
+
+        @pl.loop(0, CAPACITY, unroll=4)
+        def _(s):
+            for y in range(height):
+                piece = pl.ds(y * width, width)
+                total = pre[s, piece]
+                if y == 0:
+                    total = total + rim[0, s]
+                if y == height - 1:
+                    total = total + rim[1, s]
+                z = zbuf[s, piece]
+                hid[s, piece] = (1.0 - z) * hid[s, piece] + z * jnp.tanh(total)
 
         def message(j):
             first_sum = jnp.zeros((rows, chans), F32)
@@ -299,56 +340,52 @@
             both = jnp.concatenate([first_sum.astype(BF16), second_sum.astype(BF16)], axis=1)
             return dot(both, wmsg_s[...])
 
-        for way, start in ((LEFT, 0), (RIGHT, 2 * fd)):
-            @pl.loop(0, fd)
-            def _(j, way=way, start=start):
+        parcels = []
+        for j in range(fd):
+            for way, start in ((LEFT, 0), (RIGHT, 2 * fd)):
                 msend[k, way, j] = message(start + j).astype(BF16)
-
-            push(base + 4 + way, way, msend.at[k, way], mrecv.at[k, way])
-
-        @pl.loop(0, fd)
-        def _(j):
+                parcels.append(push(way, msend.at[k, way, j], mrecv.at[k, way, j]))
+        for j in range(fd):
             mown[j] = message(fd + j)
-
-        for way in (LEFT, RIGHT):
-            arrive(base + 4 + way, way, msend.at[k, way], mrecv.at[k, way])
-
-        @pl.loop(0, fd)
-        def _(j):
+        for handle in parcels:
+            arrive(handle)
+        for j in range(fd):
             total = mown[j] + mrecv[k, LEFT, j].astype(F32) + mrecv[k, RIGHT, j].astype(F32)
             ubuf[k, j, pl.ds(1, height)] = (
                 jnp.maximum(total, 0.0).astype(BF16).reshape(height, width, chans)
             )
-
-        for n, side in enumerate((UP, DOWN)):
-            push(base + 8 + n, side, ubuf.at[k, :, halo_src[side]], ubuf.at[k, :, halo_dst[side]])
-        for n, side in enumerate((UP, DOWN)):
-            arrive(base + 8 + n, side, ubuf.at[k, :, halo_src[side]], ubuf.at[k, :, halo_dst[side]])
-
-        @pl.loop(0, fd)
-        def _(j):
-            acc = None
-            for dy in range(3):
-                term = dot(ubuf[k, j, pl.ds(dy, height)].reshape(rows, chans), wres_s[dy])
-                acc = term if acc is None else acc + term
-            old = cwin[k, fd + j].reshape(rows, chans).astype(F32)
-            new = (old + shifted_sum(acc)).astype(BF16).reshape(height, width, chans)
-            if k == ROUNDS - 1:
-                out_ref[j] = new
-            else:
-                sbuf[k, j] = new
-                cwin[k + 1, fd + j] = new
-
-        if k < ROUNDS - 1:
-            for way in (RIGHT, LEFT):
-                push(base + 12 + way, way, sbuf.at[k], cwin.at[k + 1, place[way]])
-            for way in (RIGHT, LEFT):
-                arrive(base + 12 + way, way, sbuf.at[k], cwin.at[k + 1, place[way]])
-
-    for i, way, src, dst, cond in sent:
-        @pl.when(cond)
-        def _(i=i, way=way, src=src, dst=dst):
-            rcopy(i, way, src, dst).wait_send()
+        halos = [
+            push(side, ubuf.at[k, :, halo_src[side]], ubuf.at[k, :, halo_dst[side]])
+            for side in (UP, DOWN)
+        ]
+        for j in range(fd):
+            part = ubuf[k, j, pl.ds(1, height)].reshape(rows, chans)
+            mown[j] = cwin[k, fd + j].reshape(rows, chans).astype(F32) + conv_own(part, wres_s)
+        for handle in halos:
+            arrive(handle)
+        states = []
+        for j in range(fd):
+            top = shifted_sum(dot(ubuf[k, j, 0], wres_s[0]))
+            bottom = shifted_sum(dot(ubuf[k, j, height + 1], wres_s[2]))
+            for y in range(height):
+                total = mown[j, y * width : (y + 1) * width]
+                if y == 0:
+                    total = total + top
+                if y == height - 1:
+                    total = total + bottom
+                if k == ROUNDS - 1:
+                    out_ref[j, y] = total.astype(BF16)
+                else:
+                    sbuf[k, j, y] = total.astype(BF16)
+                    cwin[k + 1, fd + j, y] = total.astype(BF16)
+            if k < ROUNDS - 1:
+                for way in (RIGHT, LEFT):
+                    states.append(push(way, sbuf.at[k, j], cwin.at[k + 1, seat[way] + j]))
+
+    for handle in sent:
+        @pl.when(both(has[handle[1]], handle[4]))
+        def _(handle=handle):
+            rcopy(handle).wait_send()
 
 
 def local(nf, nr, fmap, context, pairs, w_corr, w_zr, w_q, w_msg, w_res):
@@ -356,11 +393,15 @@
     rows = height * width
     win = 3 * fd
     groups = -(-(2 * RADIUS + 1) // (LANES // width))
+    copies = 6 * fd + 4 + ROUNDS * (6 + 2 * fd) + (ROUNDS - 1) * 2 * fd
     vmem = pl.BlockSpec(memory_space=pltpu.VMEM)
+    hbm = pl.BlockSpec(memory_space=pl.ANY)
     return pl.pallas_call(
         functools.partial(kernel, nf, nr),
         out_shape=jax.ShapeDtypeStruct(fmap.shape, BF16),
-        in_specs=[pl.BlockSpec(memory_space=pltpu.SMEM)] + [vmem] * 7,
+        in_specs=[
+            pl.BlockSpec(memory_space=pltpu.SMEM), vmem, vmem, vmem, vmem, hbm, vmem, hbm,
+        ],
         out_specs=vmem,
         scratch_shapes=[
             pltpu.VMEM((win, 2 * RADIUS + height + 1, width, chans), BF16),
@@ -379,10 +420,12 @@
             pltpu.VMEM((3, 2 * chans, 3 * chans), BF16),
             pltpu.VMEM((3, chans, 3 * chans), BF16),
             pltpu.VMEM((2 * chans, chans), BF16),
+            pltpu.VMEM((CAPACITY, rows, chans), F32),
+            pltpu.VMEM((2, CAPACITY, width, chans), F32),
             pltpu.SMEM((4, CAPACITY), jnp.int32),
-            pltpu.SemaphoreType.DMA((16 + 16 * ROUNDS,)),
-            pltpu.SemaphoreType.DMA((16 + 16 * ROUNDS,)),
-            pltpu.SemaphoreType.DMA((2,)),
+            pltpu.SemaphoreType.DMA((copies,)),
+            pltpu.SemaphoreType.DMA((copies,)),
+            pltpu.SemaphoreType.DMA((20,)),
         ],
         compiler_params=pltpu.CompilerParams(collective_id=0, has_side_effects=True),
     )(pairs, fmap, context, w_corr, w_zr, w_q, w_msg, w_res)

time: 64.8 us -> 56.6 us (0.87)
  Pallas kernels: 61.7 us -> 53.5 us
    pallas_call x1, Pallas kernels: 61.7 us -> 53.5 us  [local(): pl.pallas_call(functools.partial(kernel, nf, nr), out_shape=jax.ShapeDtyp...]
where the time goes in v2:
time: 56.6 us; the launch traced here: 56.4 us
  Pallas kernels  53.5 us (95%)
  local copies, waits for them, and re-layouts  2.91 us (5%)
    pallas_call x1, Pallas kernels, local(): pl.pallas_call(functools.partial(kernel, nf, nr), out_shape=jax.ShapeDtyp...  53.5 us
    unnamed x2, local copies, waits for them, and re-layouts  2.91 us

profile of v2, /device:TPU:9, one launch (start us, length us, event | category | flops | bytes accessed | tf_op | source)
XLA Modules:
  0.0 56.4 jit_solution(12639979147344346604)
XLA Ops:
  0.0 1.4 %copy.9.pairs_ref = s32[32,3]{1,0:T(8,128)} copy(s32[32,3]{0,1:T(4,128)} %param.10) | data formatting | bytes 768 | tf_op args[2]
  1.4 53.5 %shard_map.82 = bf16[2,3,64,128]{3,2,1,0:T(8,128)(2,1)} custom-call(s32[32,3]{1,0:T(8,128)} %copy.9.pairs_ref, bf16[2,3,64,128]{3,2,1,0:T(8,128)(2,1)} %fmap_ref.1, bf16[2,3,64,128]{3,2,1,0:T(8,128)(2,1)} %ctx_ref.1, bf16[49,128]{1,0:T(8,128)(2,1)} %wcorr_ref.1, bf16[256,256]{1,0:T(8,128)(2,1)} %wzr_ref.1, bf16[9,256,128]{2,1,0:T(8,128)(2,1)} %wq_ref.1, ...), custom_call_target="tpu_custom_call" | custom-call | tf_op jit(solution)/shard_map/pallas_call | solution.py:399
  54.8 1.5 %copy.11 = bf16[2,3,64,128]{3,2,1,0:T(8,128)(2,1)} copy(bf16[2,3,64,128]{3,2,1,0:T(8,128)(2,1)} %shard_map.82) | data formatting | bytes 196608
